TPU v7x, 32 devices: a whole 2x2x4 slice. The times are simulated.
32 devices in a mesh: member: 4 (over y, x), space: 8 (over z, core).
Axes of the slice: x: 2, y: 2, z: 4, core: 2. Of those that a mesh axis runs over, the one named last changes fastest.
Arguments:
- ensemble_prediction: bfloat16 [4, 300, 128, 128], P('member', None, 'space'), may hold values from -6 to 6
- observed_analysis: bfloat16 [300, 128, 128], P(None, 'space'), may hold values from -6 to 6
- validity_flags: int32 [2, 128, 128], P(None, 'space'), may hold values from 0 to 1, as said below
Outputs:
- point_score: float32 [300, 128, 128], P(None, 'space')
- channel_loss: float32 [300], replicated
Inputs may be any that keep to these rules, and one draw needn't show every extreme that they name: `validity_flags`: 0 or 1 for each point and group; every point of latitude row 11 is valid in both groups.
All inputs are finite; a program needn't handle non-finite values.
Results may differ from a plain program's by a relative error of at most 0.0003.
Values may be sent and summed in bfloat16 or wider, within the bound.
A program may use at most 64 MiB of HBM per device.

v0:
```python
import jax
import jax.numpy as jnp
from jax import lax
from jax.sharding import PartitionSpec as P

VARIABLE_NUMBER = 300
ATMOS = 180
TILE_SITES = 128
LON = 720
ROWS = 360


def per_channel(values):
    is_ocean = jnp.arange(VARIABLE_NUMBER, dtype=jnp.int32) >= ATMOS
    return jnp.where(is_ocean, values[1], values[0])


def shards(ensemble_prediction, observed_analysis, validity_flags):
    blocks_here = observed_analysis.shape[1]
    realization_entries = lax.axis_size("member")
    lat_rows = min(ROWS, blocks_here * lax.axis_size("space") * TILE_SITES // LON)
    first_point = lax.axis_index("space") * (blocks_here * TILE_SITES)
    position = first_point + jnp.arange(blocks_here * TILE_SITES, dtype=jnp.int32).reshape(
        blocks_here, TILE_SITES
    )
    inside = (position < lat_rows * LON).astype(jnp.float32)
    lat_row = (position // LON).astype(jnp.float32)
    cosine = jnp.cos(jnp.pi * ((lat_row + 0.5) / lat_rows - 0.5))
    valid = inside[None] * (validity_flags > 0).astype(jnp.float32)
    weight = cosine[None] * valid
    local_area = jnp.sum(weight, axis=(1, 2))
    local_count = jnp.sum(valid, axis=(1, 2))
    is_ocean = jnp.arange(VARIABLE_NUMBER, dtype=jnp.int32) >= ATMOS
    weight_chan = jnp.where(is_ocean[:, None, None], weight[1][None], weight[0][None])
    coeff = (1.0 - 0.05 / realization_entries) / (
        2.0 * realization_entries * (realization_entries - 1)
    )
    gathered = lax.all_to_all(
        ensemble_prediction, "member", split_axis=2, concat_axis=0, tiled=True
    )
    share = blocks_here // realization_entries
    first_block = lax.axis_index("member") * share
    target_part = lax.dynamic_slice_in_dim(observed_analysis, first_block, share, 1).astype(
        jnp.float32
    )
    accuracy_component = jnp.zeros(target_part.shape, jnp.float32)
    dispersion_component = jnp.zeros(target_part.shape, jnp.float32)
    for leading_realization in range(realization_entries):
        lead = gathered[leading_realization].astype(jnp.float32)
        accuracy_component = accuracy_component + jnp.abs(lead - target_part)
        for trailing_realization in range(leading_realization + 1, realization_entries):
            dispersion_component = dispersion_component + jnp.abs(
                lead - gathered[trailing_realization].astype(jnp.float32)
            )
    partial_crps = accuracy_component / realization_entries - coeff * (2.0 * dispersion_component)
    crps = lax.all_gather(partial_crps, "member", axis=1, tiled=True)
    area_sum, count = lax.psum((local_area, local_count), "space")
    scale_chan = per_channel(count / area_sum)
    point_score = crps * weight_chan * scale_chan[:, None, None]
    score_sums = lax.psum(jnp.sum(point_score, axis=(1, 2)), "space")
    channel_loss = score_sums / per_channel(count)
    return (point_score, channel_loss)


def solution(mesh):
    in_specs = (P("member", None, "space", None), P(None, "space", None), P(None, "space", None))
    out_specs = (P(None, "space", None), P())
    return jax.shard_map(shards, mesh=mesh, in_specs=in_specs, out_specs=out_specs, check_vma=False)
```

profile of v0, /device:TPU:0, one launch (start us, length us, event | category | flops | bytes accessed | tf_op | source)
XLA Modules:
  0.0 100.8 jit_solution(2808371847547564155)
XLA Ops:
  7.2 0.0 copy-start
  7.2 2.7 %copy.11 = bf16[1,300,16,128]{3,1,0,2:T(8,128)(2,1)} copy(bf16[1,300,16,128]{3,2,1,0:T(8,128)(2,1)} %param.3) | data formatting | bytes 2457600 | tf_op args[0]
  9.9 0.0 copy-start.1
  9.9 5.3 %all-to-all-start = ((bf16[1,300,16,128]{3,1,0,2:T(8,128)(2,1)}), bf16[1,300,16,128]{3,1,0,2:T(8,128)(2,1)S(1)}, u32[]{:S(2)}, u32[]{:S(2)}) async-start(bf16[1,300,16,128]{3,1,0,2:T(8,128)(2,1)} %copy.11), calls=%async_computation | async-start | bytes 2490368 | tf_op jit(solution)/shard_map/all_to_all | solution.py:38
  15.2 0.0 all-gather.2.cloned.1.call-start
  15.2 0.0 copy-done
  15.2 0.2 constant_dynamic-slice_fusion
  15.4 15.6 %all-to-all-done = bf16[1,300,16,128]{3,1,0,2:T(8,128)(2,1)S(1)} async-done(((bf16[1,300,16,128]{3,1,0,2:T(8,128)(2,1)}), bf16[1,300,16,128]{3,1,0,2:T(8,128)(2,1)S(1)}, u32[]{:S(2)}, u32[]{:S(2)}) %all-to-all-start) | async-done | bytes 1228832 | tf_op jit(solution)/shard_map/all_to_all | solution.py:38
  31.0 1.6 %fusion.5 = f32[300,4,128]{2,0,1:T(8,128)} fusion(bf16[4,1,300,4,128]{4,2,3,0,1:T(8,128)(2,1)S(1)} %bitcast.33, bf16[4,1,300,4,128]{4,2,3,1,0:T(8,128)(2,1)S(1)} %bitcast.34, bf16[300,4,128]{2,1,0:T(4,128)(2,1)S(1)} %constant_dynamic-slice_fusion), kind=kLoop, calls=%fused_computation.16 | loop fusion | flops 5529600 | bytes 2150400 | tf_op jit(solution)/shard_map/sub | solution.py:55
  32.5 0.0 all-gather.2.cloned.1.call-update
  32.6 0.1 fusion.26
  32.7 0.0 copy-done.1
  32.7 0.1 fusion.31
  32.8 0.1 select_reduce_fusion
  32.9 15.9 %all-reduce = (f32[2]{0:T(128)S(1)}, f32[2]{0:T(128)S(1)}) all-reduce(f32[2]{0:T(128)S(1)} %select_reduce_fusion, f32[2]{0:T(128)S(1)} %get-tuple-element.10), channel_id=1, replica_groups=mesh['member'=4,'space'=8] {'space'}, use_global_device_ids=true, to_apply=%region_1.2 | all-reduce | flops 4 | bytes 32 | tf_op jit(solution)/shard_map/psum | solution.py:57
  48.8 0.6 fusion.33
  49.4 1.3 %broadcast_select_fusion = f32[300]{0:T(512)S(1)} fusion(f32[]{:T(128)} %bitcast.16, f32[]{:T(128)} %bitcast.15), kind=kLoop, calls=%fused_computation.56 | loop fusion | flops 600 | bytes 1208 | tf_op jit(solution)/shard_map/jit(_where)/select_n | solution.py:15
  50.7 0.6 fusion.32
  51.3 20.2 %all-gather.2.cloned.1.call-done = f32[300,16,128]{2,0,1:T(8,128)} async-done(((f32[300,4,128]{2,0,1:T(8,128)}), f32[300,16,128]{2,0,1:T(8,128)}) %all-gather.2.cloned.1.call-update) | async-done | bytes 2457616 | tf_op jit(solution)/shard_map/all_gather | solution.py:56
  71.5 2.2 %fusion.30 = (f32[300]{0:T(512)S(1)}, f32[300,16,128]{2,0,1:T(8,128)S(1)}) fusion(f32[300]{0:T(512)S(1)} %broadcast_select_fusion, f32[300,16,128]{2,0,1:T(8,128)} %all-gather.2.cloned.1.call-done, f32[16,128]{1,0:T(8,128)S(1)} %get-tuple-element.14, f32[16,128]{1,0:T(8,128)S(1)} %get-tuple-element.13, pred[300]{0:T(512)(128)(4,1)S(1)} %iota_compare_fusion), kind=kLoop, calls=%fused_computation.58 | loop fusion | flops 2457300 | bytes 4934284 | tf_op jit(solution)/shard_map/reduce_sum | solution.py:60
  73.7 2.2 %copy.16 = f32[300,16,128]{2,1,0:T(8,128)} copy(f32[300,16,128]{2,0,1:T(8,128)S(1)} %get-tuple-element.9) | data formatting | bytes 4915200
  75.9 16.2 %psum.23 = f32[300]{0:T(512)S(1)} all-reduce(f32[300]{0:T(512)S(1)} %get-tuple-element.8), channel_id=1, replica_groups=mesh['member'=4,'space'=8] {'space'}, use_global_device_ids=true, to_apply=%region_5.6 | all-reduce | flops 300 | bytes 2400 | tf_op jit(solution)/shard_map/psum | solution.py:60
  92.1 1.9 %select_divide_fusion = f32[300]{0:T(512)} fusion(f32[300]{0:T(512)S(1)} %psum.23, f32[]{:T(128)} %bitcast.18, f32[]{:T(128)} %bitcast.17), kind=kLoop, calls=%fused_computation.54 | loop fusion | flops 900 | bytes 2408 | tf_op jit(solution)/shard_map/div | solution.py:61
  (4 shorter events, 0.0 us)
Async XLA Ops:
  7.2 8.1 %copy-start = (bf16[300,16,128]{2,1,0:T(8,128)(2,1)S(1)}, bf16[300,16,128]{2,1,0:T(8,128)(2,1)}, u32[]{:S(2)}) copy-start(bf16[300,16,128]{2,1,0:T(8,128)(2,1)} %param.4) | copy-start | bytes 3686404
  9.9 22.7 %copy-start.1 = (s32[2,16,128]{2,1,0:T(8,128)S(1)}, s32[2,16,128]{2,1,0:T(8,128)}, u32[]{:S(2)}) copy-start(s32[2,16,128]{2,1,0:T(8,128)} %param.5) | copy-start | bytes 49156
  9.9 21.1 %all-to-all-start = ((bf16[1,300,16,128]{3,1,0,2:T(8,128)(2,1)}), bf16[1,300,16,128]{3,1,0,2:T(8,128)(2,1)S(1)}, u32[]{:S(2)}, u32[]{:S(2)}) async-start(bf16[1,300,16,128]{3,1,0,2:T(8,128)(2,1)} %copy.11), calls=%async_computation | async-start | bytes 2490368 | tf_op jit(solution)/shard_map/all_to_all | solution.py:38
  15.2 56.2 %all-gather.2.cloned.1.call-start = ((), (), s32[]{:S(2)}) async-start(), calls=%async_computation.1 | async-start | bytes 3112960 | tf_op jit(solution)/shard_map/all_gather | solution.py:56
Sparse Core Ops, SparseCore 0:
  32.7 38.7 all-gather.1
where the time goes:
time: 101 us
  waiting for transfers between devices  35.8 us (35%)
  blocking collectives  32.1 us (32%)
  between operations  14.1 us (14%)
  other arithmetic  7.25 us (7%)
  local copies, waits for them, and re-layouts  6.33 us (6%)
  starting transfers between devices  5.33 us (5%)
    all_gather x1, waiting for transfers between devices, shards(): crps = lax.all_gather(partial_crps, 'member', axis=1, tiled=True)  20.2 us
    psum x1, blocking collectives, shards(): score_sums = lax.psum(jnp.sum(point_score, axis=(1, 2)), 'space')  16.2 us
    psum x1, blocking collectives, shards(): area_sum, count = lax.psum((local_area, local_count), 'space')  15.9 us
    all_to_all x1, waiting for transfers between devices, shards(): lax.all_to_all(ensemble_prediction, 'member', split_axis=2, concat_axis=0...  15.6 us
    all_to_all x1, starting transfers between devices, shards(): lax.all_to_all(ensemble_prediction, 'member', split_axis=2, concat_axis=0...  5.32 us
    unnamed x6, local copies, waits for them, and re-layouts  4.95 us
    reduce_sum x1, other arithmetic, shards(): score_sums = lax.psum(jnp.sum(point_score, axis=(1, 2)), 'space')  2.23 us
  transfers between devices with their start and end apart: 2, of which 2 were waited for; matrix products, arithmetic and copies ran while one was open for 3% of the time, Pallas kernels for 0%

commit v1 on v0

--- a/solution.py
+++ b/solution.py
@@ -53,7 +53,9 @@
                 lead - gathered[trailing_realization].astype(jnp.float32)
             )
     partial_crps = accuracy_component / realization_entries - coeff * (2.0 * dispersion_component)
-    crps = lax.all_gather(partial_crps, "member", axis=1, tiled=True)
+    crps = jnp.concatenate(
+        lax.all_to_all(jnp.stack([partial_crps] * lax.axis_size("member")), "member", 0, 0), axis=1
+    )
     area_sum, count = lax.psum((local_area, local_count), "space")
     scale_chan = per_channel(count / area_sum)
     point_score = crps * weight_chan * scale_chan[:, None, None]

time: 101 us -> 88.7 us (0.88)
  between operations: 14.1 us -> 0.71 us
  waiting for transfers between devices: 35.8 us -> 25.1 us
  starting transfers between devices: 5.33 us -> 9.83 us
  local copies, waits for them, and re-layouts: 6.33 us -> 10.2 us
  other arithmetic: 7.25 us -> 10.5 us
    all_gather x1 -> x0, waiting for transfers between devices: 20.2 us -> none  [shards(): crps = lax.all_gather(partial_crps, 'member', axis=1, tiled=True)]
    all_to_all x0 -> x1, waiting for transfers between devices: none -> 9.56 us  [shards(): lax.all_to_all(jnp.stack([partial_crps] * lax.axis_size('member')), 'memb...]
    all_to_all x0 -> x1, starting transfers between devices: none -> 4.64 us  [shards(): lax.all_to_all(jnp.stack([partial_crps] * lax.axis_size('member')), 'memb...]
    reduce_sum x1, other arithmetic: 2.23 us -> 5.98 us  [shards(): score_sums = lax.psum(jnp.sum(point_score, axis=(1, 2)), 'space')]
    reshape x0 -> x1, local copies, waits for them, and re-layouts: none -> 1.86 us  [shards(): jnp.concatenate(lax.all_to_all(jnp.stack([partial_crps] * lax.axis_size('...]
    another operation x0 -> x1, local copies, waits for them, and re-layouts: none -> 1.75 us  [shards(): jnp.stack([partial_crps] * lax.axis_size('member'))]
where the time goes in v1:
time: 88.7 us; the launch traced here: 88.2 us
  blocking collectives  31.8 us (36%)
  waiting for transfers between devices  25.1 us (28%)
  other arithmetic  10.5 us (12%)
  local copies, waits for them, and re-layouts  10.2 us (11%)
  starting transfers between devices  9.83 us (11%)
    psum x1, blocking collectives, shards(): score_sums = lax.psum(jnp.sum(point_score, axis=(1, 2)), 'space')  15.9 us
    psum x1, blocking collectives, shards(): area_sum, count = lax.psum((local_area, local_count), 'space')  15.9 us
    all_to_all x1, waiting for transfers between devices, shards(): lax.all_to_all(ensemble_prediction, 'member', split_axis=2, concat_axis=0...  15.6 us
    all_to_all x1, waiting for transfers between devices, shards(): lax.all_to_all(jnp.stack([partial_crps] * lax.axis_size('member')), 'memb...  9.56 us
    reduce_sum x1, other arithmetic, shards(): score_sums = lax.psum(jnp.sum(point_score, axis=(1, 2)), 'space')  5.98 us
    all_to_all x1, starting transfers between devices, shards(): lax.all_to_all(ensemble_prediction, 'member', split_axis=2, concat_axis=0...  5.19 us
    unnamed x6, local copies, waits for them, and re-layouts  4.94 us
    all_to_all x1, starting transfers between devices, shards(): lax.all_to_all(jnp.stack([partial_crps] * lax.axis_size('member')), 'memb...  4.64 us
  transfers between devices with their start and end apart: 2, of which 2 were waited for; matrix products, arithmetic and copies ran while one was open for 3% of the time, Pallas kernels for 0%

profile of v1, /device:TPU:0, one launch (start us, length us, event | category | flops | bytes accessed | tf_op | source)
XLA Modules:
  0.0 88.2 jit_solution(16575185337014243346)
XLA Ops:
  0.6 0.0 copy-start
  0.6 2.7 %copy.17 = bf16[1,300,16,128]{3,1,0,2:T(8,128)(2,1)} copy(bf16[1,300,16,128]{3,2,1,0:T(8,128)(2,1)} %param.3) | data formatting | bytes 2457600 | tf_op args[0]
  3.4 5.2 %all-to-all-start = ((bf16[1,300,16,128]{3,1,0,2:T(8,128)(2,1)}), bf16[1,300,16,128]{3,1,0,2:T(8,128)(2,1)S(1)}, u32[]{:S(2)}, u32[]{:S(2)}) async-start(bf16[1,300,16,128]{3,1,0,2:T(8,128)(2,1)} %copy.17), calls=%async_computation | async-start | bytes 2490368 | tf_op jit(solution)/shard_map/all_to_all | solution.py:38
  8.6 0.0 copy-done
  8.6 0.2 constant_dynamic-slice_fusion
  8.7 15.6 %all-to-all-done = bf16[1,300,16,128]{3,1,0,2:T(8,128)(2,1)S(1)} async-done(((bf16[1,300,16,128]{3,1,0,2:T(8,128)(2,1)}), bf16[1,300,16,128]{3,1,0,2:T(8,128)(2,1)S(1)}, u32[]{:S(2)}, u32[]{:S(2)}) %all-to-all-start) | async-done | bytes 1228832 | tf_op jit(solution)/shard_map/all_to_all | solution.py:38
  24.3 0.7 fusion.6
  25.0 0.2 copy.22
  25.3 1.8 %stack.2 = f32[4,300,4,128]{3,2,1,0:T(4,128)} broadcast(f32[300,4,128]{2,1,0:T(4,128)S(1)} %copy.22), dimensions={1,2,3} | broadcast | bytes 3072000 | tf_op jit(solution)/shard_map/stack | solution.py:57
  27.0 4.6 %all-to-all-start.1 = ((f32[4,300,4,128]{3,2,1,0:T(4,128)}), f32[4,300,4,128]{3,2,1,0:T(4,128)}, u32[]{:S(2)}, u32[]{:S(2)}) async-start(f32[4,300,4,128]{3,2,1,0:T(4,128)} %stack.2), calls=%async_computation.1 | async-start | bytes 4915200 | tf_op jit(solution)/shard_map/all_to_all | solution.py:57
  31.7 0.1 fusion.27
  31.8 0.1 fusion.31
  31.9 0.1 select_reduce_fusion
  32.0 15.9 %all-reduce = (f32[2]{0:T(128)S(1)}, f32[2]{0:T(128)S(1)}) all-reduce(f32[2]{0:T(128)S(1)} %select_reduce_fusion, f32[2]{0:T(128)S(1)} %get-tuple-element.6), channel_id=1, replica_groups=mesh['member'=4,'space'=8] {'space'}, use_global_device_ids=true, to_apply=%region_1.2 | all-reduce | flops 4 | bytes 32 | tf_op jit(solution)/shard_map/psum | solution.py:59
  47.9 0.6 fusion.34
  48.5 1.3 %broadcast_select_fusion = f32[300]{0:T(512)S(1)} fusion(f32[]{:T(128)} %bitcast.18, f32[]{:T(128)} %bitcast.17), kind=kLoop, calls=%fused_computation.56 | loop fusion | flops 600 | bytes 1208 | tf_op jit(solution)/shard_map/jit(_where)/select_n | solution.py:15
  49.8 0.6 fusion.33
  50.5 9.6 %all-to-all-done.1 = f32[4,300,4,128]{3,2,1,0:T(4,128)} async-done(((f32[4,300,4,128]{3,2,1,0:T(4,128)}), f32[4,300,4,128]{3,2,1,0:T(4,128)}, u32[]{:S(2)}, u32[]{:S(2)}) %all-to-all-start.1) | async-done | bytes 2457632 | tf_op jit(solution)/shard_map/all_to_all | solution.py:57
  60.0 6.0 %multiply_reduce_fusion = f32[300]{0:T(512)S(1)} fusion(f32[300]{0:T(512)S(1)} %broadcast_select_fusion, f32[4,4,128]{2,1,0:T(4,128)S(1)} %bitcast.44, f32[4,4,128]{2,1,0:T(4,128)S(1)} %bitcast.43, pred[300]{0:T(512)(128)(4,1)S(1)} %iota_compare_fusion, f32[4,300,4,128]{3,2,1,0:T(4,128)} %all-to-all-done.1), kind=kLoop, calls=%fused_computation.2 | loop fusion | flops 2457300 | bytes 2476684 | tf_op jit(solution)/shard_map/reduce_sum | solution.py:62
  66.0 15.9 %psum.23 = f32[300]{0:T(512)S(1)} all-reduce(f32[300]{0:T(512)S(1)} %multiply_reduce_fusion), channel_id=1, replica_groups=mesh['member'=4,'space'=8] {'space'}, use_global_device_ids=true, to_apply=%region_5.6 | all-reduce | flops 300 | bytes 2400 | tf_op jit(solution)/shard_map/psum | solution.py:62
  81.9 1.9 %copy.23 = f32[300,4,4,128]{3,0,2,1:T(8,128)S(1)} copy(f32[300,4,4,128]{3,2,0,1:T(4,128)} %bitcast.13) | data formatting | bytes 4915200 | tf_op jit(solution)/shard_map/reshape | solution.py:56
  83.8 0.4 fusion
  84.2 2.2 %copy.24 = f32[300,16,128]{2,1,0:T(8,128)} copy(f32[300,16,128]{2,0,1:T(8,128)S(1)} %fusion) | data formatting | bytes 4915200
  86.4 1.8 %select_divide_fusion = f32[300]{0:T(512)} fusion(f32[300]{0:T(512)S(1)} %psum.23, f32[]{:T(128)} %bitcast.22, f32[]{:T(128)} %bitcast.21), kind=kLoop, calls=%fused_computation.54 | loop fusion | flops 900 | bytes 2408 | tf_op jit(solution)/shard_map/div | solution.py:63
  (6 shorter events, 0.0 us)
Async XLA Ops:
  0.6 7.9 %copy-start = (bf16[300,16,128]{2,1,0:T(8,128)(2,1)S(1)}, bf16[300,16,128]{2,1,0:T(8,128)(2,1)}, u32[]{:S(2)}) copy-start(bf16[300,16,128]{2,1,0:T(8,128)(2,1)} %param.4) | copy-start | bytes 3686404
  3.4 20.9 %all-to-all-start = ((bf16[1,300,16,128]{3,1,0,2:T(8,128)(2,1)}), bf16[1,300,16,128]{3,1,0,2:T(8,128)(2,1)S(1)}, u32[]{:S(2)}, u32[]{:S(2)}) async-start(bf16[1,300,16,128]{3,1,0,2:T(8,128)(2,1)} %copy.17), calls=%async_computation | async-start | bytes 2490368 | tf_op jit(solution)/shard_map/all_to_all | solution.py:38
  27.0 4.7 %copy-start.1 = (s32[2,16,128]{2,1,0:T(8,128)S(1)}, s32[2,16,128]{2,1,0:T(8,128)}, u32[]{:S(2)}) copy-start(s32[2,16,128]{2,1,0:T(8,128)} %param.5) | copy-start | bytes 49156
  27.0 33.0 %all-to-all-start.1 = ((f32[4,300,4,128]{3,2,1,0:T(4,128)}), f32[4,300,4,128]{3,2,1,0:T(4,128)}, u32[]{:S(2)}, u32[]{:S(2)}) async-start(f32[4,300,4,128]{3,2,1,0:T(4,128)} %stack.2), calls=%async_computation.1 | async-start | bytes 4915200 | tf_op jit(solution)/shard_map/all_to_all | solution.py:57
